TPU v7x, 32 devices: a whole 2x2x4 slice. The times are simulated.
32 devices in a mesh: rows: 8 (over z, y), feat: 4 (over x, core).
Axes of the slice: x: 2, y: 2, z: 4, core: 2. Of those that a mesh axis runs over, the one named last changes fastest.
Arguments:
- cells: bfloat16 [1024, 80, 128], P('rows', 'feat'), may hold values from -19 to 19
- block_table: int32 [8], replicated, may hold values from 0 to 7, as said below
- row_live: int32 [1024], replicated, may hold values from 0 to 1, as said below
- row_train: int32 [1024], replicated, may hold values from 0 to 1, as said below
- feat_qkv: bfloat16 [128, 384], replicated, may hold values from -0.5 to 0.5
- feat_out: bfloat16 [128, 128], replicated, may hold values from -0.5 to 0.5
- item_qkv: bfloat16 [128, 384], replicated, may hold values from -0.5 to 0.5
- item_out: bfloat16 [128, 128], replicated, may hold values from -0.5 to 0.5
Outputs:
- layer_output: bfloat16 [1024, 80, 128], P(('rows', 'feat'))
Inputs may be any that keep to these rules, and one draw needn't show every extreme that they name: `block_table`: every table number appears in some block. `row_live`: every training row is live. `row_train`: each aligned group of 32 rows holds 1 to 4 training rows; some group holds exactly 4.
All inputs are finite; a program needn't handle non-finite values.
Results may differ from a plain program's by a relative error of at most 0.014.
Values may be sent and summed in bfloat16 or wider, within the bound.
No kernel may reach another device: no remote copies, remote signals or barrier semaphores. Data moves between devices by JAX's collectives and lax.ppermute only.
A program may use at most 64 MiB of HBM per device.

v0:
```python
import jax
import jax.numpy as jnp
from jax import lax
from jax.sharding import PartitionSpec as P

HEADS = 4
HEAD_DIM = 32
KEEP = 4
TABLES = 8
EPSILON = 1e-05
MASKED = -1e30


def compact_train(train_rows):
    positions = jnp.arange(train_rows.shape[-1], dtype=jnp.int32)
    ordinal = jnp.cumsum(train_rows, axis=-1) - 1
    slot_ids = jnp.arange(KEEP, dtype=jnp.int32)
    matched = (train_rows[..., None, :] == 1) & (ordinal[..., None, :] == slot_ids[:, None])
    return jnp.sum(jnp.where(matched, positions, 0), axis=-1)


def into_heads(tensor):
    return tensor.reshape(tensor.shape[:-1] + (HEADS, HEAD_DIM))


def attend_features(queries, key_part, value_part):
    row_count, query_feats = (queries.shape[0], queries.shape[1])
    blocks = max(1, row_count * query_feats // 1280)
    while row_count % blocks:
        blocks -= 1
    scaling = HEAD_DIM ** (-0.5)

    def attend_one_block(block_parts):
        block_query, block_key, block_value = block_parts
        scores = (
            jnp.einsum(
                "rqhd,rkhd->rhqk", block_query, block_key, preferred_element_type=jnp.float32
            )
            * scaling
        )
        shares = jax.nn.softmax(scores, axis=-1).astype(jnp.bfloat16)
        return jnp.einsum(
            "rhqk,rkhd->rqhd", shares, block_value, preferred_element_type=jnp.float32
        ).astype(jnp.bfloat16)

    def by_block(tensor):
        return tensor.reshape((blocks, row_count // blocks) + tensor.shape[1:])

    result = lax.map(
        attend_one_block, (by_block(queries), by_block(key_part), by_block(value_part))
    )
    return result.reshape(row_count, query_feats, HEADS * HEAD_DIM)


def feature_layer(normed_cells, feat_out, key_part, value_part, queries):
    attended = attend_features(queries, key_part, value_part)
    update = jnp.dot(attended, feat_out, preferred_element_type=jnp.float32)
    return (normed_cells.astype(jnp.float32) + update).astype(jnp.bfloat16)


def on_device(cells, block_table, row_live, row_train, feat_qkv, feat_out, item_qkv, item_out):
    rows_here, feats_here, width_all = cells.shape
    row_index = lax.axis_index("rows")
    feat_index = lax.axis_index("feat")
    row_devices = lax.axis_size("rows")
    feat_devices = lax.axis_size("feat")
    my_table = lax.dynamic_index_in_dim(block_table, row_index, keepdims=False)
    live_rows = lax.dynamic_slice_in_dim(row_live, row_index * rows_here, rows_here).astype(
        jnp.float32
    )
    values = cells.astype(jnp.float32)
    table_hot = (jnp.arange(TABLES, dtype=jnp.int32) == my_table).astype(jnp.float32)
    first_local = jnp.sum(values * live_rows[:, None, None], axis=(0, 2))
    count_local = jnp.sum(live_rows) * width_all
    first_sum, count_sum = lax.psum(
        (table_hot[:, None] * first_local[None, :], table_hot * count_local), "rows"
    )
    table_mean = first_sum / count_sum[:, None]
    mine_mean = lax.dynamic_index_in_dim(table_mean, my_table, keepdims=False)
    centred = values - mine_mean[None, :, None]
    second_local = jnp.sum(centred * centred * live_rows[:, None, None], axis=(0, 2))
    second_sum = lax.psum(table_hot[:, None] * second_local[None, :], "rows")
    table_spread = second_sum / count_sum[:, None]
    mine_spread = lax.dynamic_index_in_dim(table_spread, my_table, keepdims=False)
    normed = (centred * lax.rsqrt(mine_spread + EPSILON)[None, :, None]).astype(jnp.bfloat16)
    normed_rows = lax.all_to_all(normed, "feat", split_axis=0, concat_axis=1, tiled=True)
    projected = jnp.dot(normed_rows, feat_qkv, preferred_element_type=jnp.float32).astype(
        jnp.bfloat16
    )
    queries = into_heads(projected[..., :width_all])
    key_part = into_heads(projected[..., width_all : 2 * width_all])
    value_part = into_heads(projected[..., 2 * width_all :])
    mixed_rows = feature_layer(normed_rows, feat_out, key_part, value_part, queries)
    group_rows, total_feats = (mixed_rows.shape[0], mixed_rows.shape[1])
    per_device = total_feats * HEADS // row_devices
    first_row = row_index * rows_here + feat_index * group_rows
    train_here = lax.dynamic_slice_in_dim(row_train, first_row, group_rows)
    places = compact_train(train_here)
    chosen = jnp.take(mixed_rows, places, axis=0)
    item_query = jnp.dot(
        mixed_rows, item_qkv[:, :width_all], preferred_element_type=jnp.float32
    ).astype(jnp.bfloat16)
    item_query = item_query.reshape(group_rows, row_devices, per_device, HEAD_DIM)
    key_value = jnp.dot(chosen, item_qkv[:, width_all:], preferred_element_type=jnp.float32).astype(
        jnp.bfloat16
    )
    item_key = key_value[..., :width_all].reshape(KEEP, row_devices, per_device, HEAD_DIM)
    item_value = key_value[..., width_all:].reshape(KEEP, row_devices, per_device, HEAD_DIM)
    query_table = jnp.repeat(block_table, group_rows)
    groups_all = row_train.reshape(row_devices, feat_devices, group_rows)
    group_counts = jnp.sum(groups_all, axis=2)
    slot_ids = jnp.arange(KEEP, dtype=jnp.int32)
    key_valid = slot_ids[None, None, :] < jnp.transpose(group_counts)[:, :, None]
    key_table = jnp.broadcast_to(block_table[None, :, None], key_valid.shape)
    allowed = (query_table[:, None] == key_table.reshape(-1)[None, :]) & key_valid.reshape(-1)[
        None, :
    ]
    query_count = query_table.shape[0]
    key_count = allowed.shape[1]
    query_blocks = max(1, query_count // 512)
    while query_count % query_blocks:
        query_blocks -= 1
    scaling = HEAD_DIM ** (-0.5)
    blocked_allowed = allowed.reshape(query_blocks, query_count // query_blocks, key_count)
    local_query = lax.all_to_all(item_query, "rows", split_axis=1, concat_axis=0, tiled=True)
    local_key = lax.all_to_all(item_key, "rows", split_axis=1, concat_axis=0, tiled=True)
    local_value = lax.all_to_all(item_value, "rows", split_axis=1, concat_axis=0, tiled=True)
    every_key = lax.all_gather(local_key, "feat", axis=0, tiled=True)
    every_value = lax.all_gather(local_value, "feat", axis=0, tiled=True)

    def one_item(item_parts):
        single_query, single_key, single_value = item_parts

        def one_one_block(block_parts):
            block_query, block_allowed = block_parts
            scores = (
                jnp.dot(block_query, single_key.T, preferred_element_type=jnp.float32) * scaling
            )
            scores = jnp.where(block_allowed, scores, MASKED)
            shares = jax.nn.softmax(scores, axis=-1).astype(jnp.bfloat16)
            return jnp.dot(shares, single_value, preferred_element_type=jnp.float32).astype(
                jnp.bfloat16
            )

        blocked_query = single_query.reshape(query_blocks, query_count // query_blocks, HEAD_DIM)
        return lax.map(one_one_block, (blocked_query, blocked_allowed)).reshape(
            query_count, HEAD_DIM
        )

    by_item = (
        jnp.moveaxis(local_query[:, 0], 1, 0),
        jnp.moveaxis(every_key[:, 0], 1, 0),
        jnp.moveaxis(every_value[:, 0], 1, 0),
    )
    result = jnp.moveaxis(lax.map(one_item, by_item), 0, 1)[:, None]
    attended = lax.all_to_all(result, "rows", split_axis=0, concat_axis=1, tiled=True)
    attended = attended.reshape(group_rows, total_feats, width_all)
    update = jnp.dot(attended, item_out, preferred_element_type=jnp.float32)
    return (mixed_rows.astype(jnp.float32) + update).astype(jnp.bfloat16)


def solution(mesh):
    return jax.shard_map(
        on_device,
        mesh=mesh,
        in_specs=(P("rows", "feat", None), P(), P(), P(), P(), P(), P(), P()),
        out_specs=P(("rows", "feat"), None, None),
        check_vma=False,
    )
```

profile of v0, /device:TPU:0, one launch (start us, length us, event | category | flops | bytes accessed | tf_op | source)
XLA Modules:
  0.0 317.5 jit_solution(12919230653871559837)
XLA Ops:
  7.2 23.4 %all-reduce = (f32[8,20]{1,0:T(8,128)S(1)}, f32[8]{0:T(128)S(1)}) all-reduce(f32[8,20]{1,0:T(8,128)S(1)} %broadcast_multiply_fusion.1, f32[8]{0:T(128)S(1)} %compare_select_fusion.2), channel_id=1, replica_groups=mesh['rows'=8,'feat'=4] {'rows'}, use_global_device_ids=true, to_apply=%region_1.2 | all-reduce | flops 168 | bytes 1344 | tf_op jit(solution)/shard_map/psum | solution.py:75
  31.2 1.7 fusion.38
  33.0 17.1 %psum.23 = f32[8,20]{1,0:T(8,128)S(1)} all-reduce(f32[8,20]{1,0:T(8,128)S(1)} %broadcast_multiply_fusion), channel_id=1, replica_groups=mesh['rows'=8,'feat'=4] {'rows'}, use_global_device_ids=true, to_apply=%region_5.6 | all-reduce | flops 160 | bytes 1280 | tf_op jit(solution)/shard_map/psum | solution.py:82
  50.2 2.5 fusion.39
  52.6 3.5 %all-to-all-start = ((bf16[128,20,128]{2,1,0:T(8,128)(2,1)}), bf16[128,20,128]{2,1,0:T(8,128)(2,1)S(1)}, u32[]{:S(2)}, u32[]{:S(2)}) async-start(bf16[128,20,128]{2,1,0:T(8,128)(2,1)} %fusion.39), calls=%async_computation | async-start | bytes 1572864 | tf_op jit(solution)/shard_map/all_to_all | solution.py:86
  56.7 11.0 %all-to-all-done = bf16[128,20,128]{2,1,0:T(8,128)(2,1)S(1)} async-done(((bf16[128,20,128]{2,1,0:T(8,128)(2,1)}), bf16[128,20,128]{2,1,0:T(8,128)(2,1)S(1)}, u32[]{:S(2)}, u32[]{:S(2)}) %all-to-all-start) | async-done | bytes 655392 | tf_op jit(solution)/shard_map/all_to_all | solution.py:86
  72.3 11.1 %while.25 = (s32[]{:T(128)}, bf16[2,16,80,4,32]{2,4,3,1,0:T(8,128)(2,1)}, bf16[2,16,80,4,32]{2,4,3,1,0:T(8,128)(2,1)}, bf16[2,16,80,4,32]{2,4,3,1,0:T(8,128)(2,1...) while((s32[]{:T(128)}, bf16[2,16,80,4,32]{2,4,3,1,0:T(8,128)(2,1)}, ...), condition=%wide.region_9.10_spmd, body=%wide.region_6.9_spmd.sunk | while | flops 55050320 | bytes 17553560 | solution.py:49
  72.9 3.4 %fusion.79 = (f32[16,4,80]{2,1,0:T(4,128)S(1)}, f32[16,4,80,80]{2,3,1,0:T(8,128)S(1)}) fusion(f32[16,4,80,80]{2,3,1,0:T(8,128)S(1)} %fusion.78), kind=kOutput, calls=%fused_computation.89.clone.1 | output fusion | flops 1638479 | bytes 3297280 | tf_op jit(solution)/shard_map/while/body/eval_jaxpr/sub | solution.py:41
  78.5 3.4 %fusion.79 = (f32[16,4,80]{2,1,0:T(4,128)S(1)}, f32[16,4,80,80]{2,3,1,0:T(8,128)S(1)}) fusion(f32[16,4,80,80]{2,3,1,0:T(8,128)S(1)} %fusion.78), kind=kOutput, calls=%fused_computation.89.clone.1 | output fusion | flops 1638479 | bytes 3297280 | tf_op jit(solution)/shard_map/while/body/eval_jaxpr/sub | solution.py:41
  83.4 1.9 fusion.41
  87.6 3.4 %all-to-all-start.2 = ((bf16[8,2,2560]{2,1,0:T(2,128)(2,1)}), bf16[8,2,2560]{2,1,0:T(2,128)(2,1)S(1)}, u32[]{:S(2)}, u32[]{:S(2)}) async-start(bf16[8,2,2560]{2,1,0:T(2,128)(2,1)} %reshape.214), calls=%async_computation.2 | async-start | bytes 163840 | tf_op jit(solution)/shard_map/all_to_all | solution.py:126
  92.3 5.6 %all-to-all-done.2 = bf16[8,2,2560]{2,1,0:T(2,128)(2,1)S(1)} async-done(((bf16[8,2,2560]{2,1,0:T(2,128)(2,1)}), bf16[8,2,2560]{2,1,0:T(2,128)(2,1)S(1)}, u32[]{:S(2)}, u32[]{:S(2)}) %all-to-all-start.2) | async-done | bytes 81952 | tf_op jit(solution)/shard_map/all_to_all | solution.py:126
  97.9 3.4 %all-to-all-start.3 = ((bf16[8,2,2560]{2,1,0:T(2,128)(2,1)}), bf16[8,2,2560]{2,1,0:T(2,128)(2,1)S(1)}, u32[]{:S(2)}, u32[]{:S(2)}) async-start(bf16[8,2,2560]{2,1,0:T(2,128)(2,1)} %reshape.216), calls=%async_computation.3 | async-start | bytes 163840 | tf_op jit(solution)/shard_map/all_to_all | solution.py:127
  102.4 3.1 reshape.193
  105.5 2.5 copy.118
  107.9 5.7 %reshape.212 = bf16[8,2,20480]{2,1,0:T(2,128)(2,1)} reshape(bf16[8,32,32,40]{3,2,1,0:T(8,128)(2,1)} %bitcast.134) | data formatting | bytes 1310720
  113.7 5.9 %all-to-all-start.1 = ((bf16[8,2,20480]{2,1,0:T(2,128)(2,1)}), bf16[8,2,20480]{2,1,0:T(2,128)(2,1)}, u32[]{:S(2)}, u32[]{:S(2)}) async-start(bf16[8,2,20480]{2,1,0:T(2,128)(2,1)} %reshape.212), calls=%async_computation.1 | async-start | bytes 1310720 | tf_op jit(solution)/shard_map/all_to_all | solution.py:125
  120.9 9.1 %all_gather.6 = bf16[128,1,40,32]{2,3,1,0:T(8,128)(2,1)S(1)} all-gather(bf16[32,1,40,32]{2,3,1,0:T(8,128)(2,1)S(1)} %bitcast.143), channel_id=1, replica_groups=mesh['rows'=8,'feat'=4] {'feat'}, dimensions={0}, use_global_device_ids=true | all-gather | bytes 409600 | tf_op jit(solution)/shard_map/all_gather | solution.py:128
  130.0 2.9 copy.125
  133.3 10.2 %all_gather.7 = bf16[128,1,40,32]{2,3,1,0:T(8,128)(2,1)S(1)} all-gather(bf16[32,1,40,32]{2,3,1,0:T(8,128)(2,1)S(1)} %bitcast.144), channel_id=1, replica_groups=mesh['rows'=8,'feat'=4] {'feat'}, dimensions={0}, use_global_device_ids=true | all-gather | bytes 409600 | tf_op jit(solution)/shard_map/all_gather | solution.py:129
  143.5 2.9 copy.126
  146.3 5.0 %reshape.213 = bf16[8,32,32,40]{3,2,1,0:T(8,128)(2,1)S(1)} reshape(bf16[8,2,20480]{2,1,0:T(2,128)(2,1)} %all-to-all-done.1) | data formatting | bytes 1310720
  151.4 4.9 %copy.124 = bf16[40,256,32]{2,1,0:T(8,128)(2,1)} copy(bf16[40,256,32]{0,2,1:T(8,128)(2,1)S(1)} %bitcast.135) | data formatting | bytes 1310720
  156.3 105.4 %while.26 = (s32[]{:T(128)}, bf16[40,256,32]{1,2,0:T(8,128)(2,1)}, bf16[40,256,32]{2,1,0:T(8,128)(2,1)}, bf16[40,128,32]{2,1,0:T(8,128)(2,1)}, bf16[40,128,32]{2...) while((s32[]{:T(128)}, bf16[40,256,32]{1,2,0:T(8,128)(2,1)}, ...), condition=%wide.region_16.17_spmd.clone, body=%wide.region_13.16_spmd.clone.sunk | while | flops 4529666 | bytes 549597 | solution.py:155
  261.7 4.5 %copy.127 = bf16[40,256,32]{0,2,1:T(8,128)(2,1)S(1)} copy(bf16[40,256,32]{1,2,0:T(8,128)(2,1)} %get-tuple-element.83) | data formatting | bytes 1310720 | tf_op jit(solution)/shard_map/while | solution.py:155
  266.2 1.7 bitcast_bitcast_fusion
  267.9 5.0 %reshape.218 = bf16[8,2,20480]{2,1,0:T(2,128)(2,1)S(1)} reshape(bf16[256,1,32,40]{3,2,1,0:T(8,128)(2,1)} %bitcast_bitcast_fusion) | data formatting | bytes 1310720
  273.0 24.0 %all_to_all.84 = bf16[8,2,20480]{2,1,0:T(2,128)(2,1)S(1)} all-to-all(bf16[8,2,20480]{2,1,0:T(2,128)(2,1)S(1)} %reshape.218), channel_id=1, replica_groups=mesh['rows'=8,'feat'=4] {'rows'}, dimensions={0} | all-to-all | bytes 1310720 | tf_op jit(solution)/shard_map/all_to_all | solution.py:156
  297.0 4.3 %reshape.219 = bf16[256,1,32,40]{3,2,1,0:T(8,128)(2,1)} reshape(bf16[8,2,20480]{2,1,0:T(2,128)(2,1)S(1)} %all_to_all.84) | data formatting | bytes 1310720
  301.3 5.9 %copy.135 = bf16[8,32,1,40,32]{1,0,4,3,2:T(8,128)(2,1)S(1)} copy(bf16[8,32,1,40,32]{3,4,1,0,2:T(8,128)(2,1)} %bitcast.136) | data formatting | bytes 1310720 | tf_op jit(solution)/shard_map/all_to_all | solution.py:156
  307.2 5.6 %copy.129 = bf16[32,8,1,40,32]{4,3,1,0,2:T(8,128)(2,1)} copy(bf16[32,8,1,40,32]{0,1,4,3,2:T(8,128)(2,1)S(1)} %bitcast.133) | data formatting | bytes 1310720 | tf_op jit(solution)/shard_map/all_to_all | solution.py:156
  312.8 3.6 %reshape.197 = bf16[32,80,128]{2,1,0:T(8,128)(2,1)S(1)} reshape(bf16[32,8,1,40,32]{4,3,1,0,2:T(8,128)(2,1)} %copy.129) | data formatting | bytes 1310720 | tf_op jit(solution)/shard_map/reshape | solution.py:157
  (202 shorter events, 127.8 us)
Async XLA Ops:
  0.0 68.7 %copy-start = (bf16[128,384]{1,0:T(8,128)(2,1)S(1)}, bf16[128,384]{1,0:T(8,128)(2,1)}, u32[]{:S(2)}) copy-start(bf16[128,384]{1,0:T(8,128)(2,1)} %param.16) | copy-start | bytes 294916
  7.1 49.0 %copy-start.8 = (s32[1024]{0:T(1024)S(1)}, s32[1024]{0:T(1024)}, u32[]{:S(2)}) copy-start(s32[1024]{0:T(1024)} %param.15) | copy-start | bytes 12292
  52.6 15.1 %all-to-all-start = ((bf16[128,20,128]{2,1,0:T(8,128)(2,1)}), bf16[128,20,128]{2,1,0:T(8,128)(2,1)S(1)}, u32[]{:S(2)}, u32[]{:S(2)}) async-start(bf16[128,20,128]{2,1,0:T(8,128)(2,1)} %fusion.39), calls=%async_computation | async-start | bytes 1572864 | tf_op jit(solution)/shard_map/all_to_all | solution.py:86
  67.9 0.8 copy-start.1
  72.3 11.1 %copy-start.6 = (bf16[128,128]{1,0:T(8,128)(2,1)S(1)}, bf16[128,128]{1,0:T(8,128)(2,1)}, u32[]{:S(2)}) copy-start(bf16[128,128]{1,0:T(8,128)(2,1)} %param.17) | copy-start | bytes 98308
  72.9 3.5 %copy-start.2 = (bf16[2,16,80,4,32]{2,4,3,1,0:T(8,128)(2,1)S(1)}, bf16[2,16,80,4,32]{2,4,3,1,0:T(8,128)(2,1)}, u32[]{:S(2)}) copy-start(bf16[2,16,80,4,32]{2,4,3,1,0:T(8,128)(2,1)} %get-tuple-element.284) | copy-start | bytes 1966084 | tf_op jit(solution)/shard_map/while
  72.9 3.5 %copy-start.4 = (bf16[2,16,80,4,32]{2,4,3,1,0:T(8,128)(2,1)S(1)}, bf16[2,16,80,4,32]{2,4,3,1,0:T(8,128)(2,1)}, u32[]{:S(2)}) copy-start(bf16[2,16,80,4,32]{2,4,3,1,0:T(8,128)(2,1)} %get-tuple-element.291) | copy-start | bytes 1966084 | tf_op jit(solution)/shard_map/while
  76.9 1.0 copy-start.3
  78.4 3.5 %copy-start.2 = (bf16[2,16,80,4,32]{2,4,3,1,0:T(8,128)(2,1)S(1)}, bf16[2,16,80,4,32]{2,4,3,1,0:T(8,128)(2,1)}, u32[]{:S(2)}) copy-start(bf16[2,16,80,4,32]{2,4,3,1,0:T(8,128)(2,1)} %get-tuple-element.284) | copy-start | bytes 1966084 | tf_op jit(solution)/shard_map/while
  78.4 3.5 %copy-start.4 = (bf16[2,16,80,4,32]{2,4,3,1,0:T(8,128)(2,1)S(1)}, bf16[2,16,80,4,32]{2,4,3,1,0:T(8,128)(2,1)}, u32[]{:S(2)}) copy-start(bf16[2,16,80,4,32]{2,4,3,1,0:T(8,128)(2,1)} %get-tuple-element.291) | copy-start | bytes 1966084 | tf_op jit(solution)/shard_map/while
  82.4 1.0 copy-start.3
  83.4 2.5 copy-start.5
  87.6 10.3 %all-to-all-start.2 = ((bf16[8,2,2560]{2,1,0:T(2,128)(2,1)}), bf16[8,2,2560]{2,1,0:T(2,128)(2,1)S(1)}, u32[]{:S(2)}, u32[]{:S(2)}) async-start(bf16[8,2,2560]{2,1,0:T(2,128)(2,1)} %reshape.214), calls=%async_computation.2 | async-start | bytes 163840 | tf_op jit(solution)/shard_map/all_to_all | solution.py:126
  97.9 15.8 %all-to-all-start.3 = ((bf16[8,2,2560]{2,1,0:T(2,128)(2,1)}), bf16[8,2,2560]{2,1,0:T(2,128)(2,1)S(1)}, u32[]{:S(2)}, u32[]{:S(2)}) async-start(bf16[8,2,2560]{2,1,0:T(2,128)(2,1)} %reshape.216), calls=%async_computation.3 | async-start | bytes 163840 | tf_op jit(solution)/shard_map/all_to_all | solution.py:127
  107.9 12.2 %copy-start.9 = (s32[8]{0:T(128)S(1)}, s32[8]{0:T(128)}, u32[]{:S(2)}) copy-start(s32[8]{0:T(128)} %param.13) | copy-start | bytes 100
  113.7 32.7 %all-to-all-start.1 = ((bf16[8,2,20480]{2,1,0:T(2,128)(2,1)}), bf16[8,2,20480]{2,1,0:T(2,128)(2,1)}, u32[]{:S(2)}, u32[]{:S(2)}) async-start(bf16[8,2,20480]{2,1,0:T(2,128)(2,1)} %reshape.212), calls=%async_computation.1 | async-start | bytes 1310720 | tf_op jit(solution)/shard_map/all_to_all | solution.py:125
  312.8 3.6 %copy-start.7 = (bf16[128,128]{1,0:T(8,128)(2,1)S(1)}, bf16[128,128]{1,0:T(8,128)(2,1)}, u32[]{:S(2)}) copy-start(bf16[128,128]{1,0:T(8,128)(2,1)} %param.19) | copy-start | bytes 98308
where the time goes:
time: 323 us; the launch traced here: 318 us
  matrix products  111 us (34%)
  blocking collectives  83.7 us (26%)
  local copies, waits for them, and re-layouts  69.6 us (22%)
  other arithmetic  18 us (6%)
  waiting for transfers between devices  16.6 us (5%)
  starting transfers between devices  16.1 us (5%)
    dot_general x40, matrix products, one_one_block(): jnp.dot(shares, single_value, preferred_element_type=jnp.float32)  62.3 us
    dot_general x40, matrix products, one_one_block(): jnp.dot(block_query, single_key.T, preferred_element_type=jnp.float32)  41.1 us
    unnamed x27, local copies, waits for them, and re-layouts  36.2 us
    all_to_all x1, blocking collectives, on_device(): lax.all_to_all(result, 'rows', split_axis=0, concat_axis=1, tiled=True)  24 us
    psum x1, blocking collectives, on_device(): lax.psum((table_hot[:, None] * first_local[None, :], table_hot * count_lo...  23.4 us
    psum x1, blocking collectives, on_device(): second_sum = lax.psum(table_hot[:, None] * second_local[None, :], 'rows')  17.1 us
    all_to_all x2, local copies, waits for them, and re-layouts, on_device(): lax.all_to_all(result, 'rows', split_axis=0, concat_axis=1, tiled=True)  11.5 us
    all_to_all x1, waiting for transfers between devices, on_device(): lax.all_to_all(normed, 'feat', split_axis=0, concat_axis=1, tiled=True)  11 us
  transfers between devices with their start and end apart: 4, of which 2 were waited for; matrix products, arithmetic and copies ran while one was open for 7% of the time, Pallas kernels for 0%

commit v1 on v0

--- a/solution.py
+++ b/solution.py
@@ -153,7 +153,10 @@
         jnp.moveaxis(every_value[:, 0], 1, 0),
     )
     result = jnp.moveaxis(lax.map(one_item, by_item), 0, 1)[:, None]
-    attended = lax.all_to_all(result, "rows", split_axis=0, concat_axis=1, tiled=True)
+    attended = jnp.concatenate(
+        lax.all_to_all(jnp.stack(jnp.split(result, lax.axis_size("rows"), axis=0)), "rows", 0, 0),
+        axis=1,
+    )
     attended = attended.reshape(group_rows, total_feats, width_all)
     update = jnp.dot(attended, item_out, preferred_element_type=jnp.float32)
     return (mixed_rows.astype(jnp.float32) + update).astype(jnp.bfloat16)

time: 323 us -> 288 us (0.89)
  matrix products: 111 us -> 89.1 us
  local copies, waits for them, and re-layouts: 69.6 us -> 55.7 us
    dot_general x40, matrix products: 62.3 us -> 37.9 us  [one_one_block(): jnp.dot(shares, single_value, preferred_element_type=jnp.float32)]
    all_to_all x2 -> x0, local copies, waits for them, and re-layouts: 11.5 us -> none  [on_device(): lax.all_to_all(result, 'rows', split_axis=0, concat_axis=1, tiled=True)]
    unnamed x27 -> x43, local copies, waits for them, and re-layouts: 36.2 us -> 33.2 us
  transfers between devices with their start and end apart: 4 -> 4, of which waited for: 2 -> 2; matrix products, arithmetic and copies ran while one was open for 7% -> 8% of each run, Pallas kernels for 0% -> 0%
where the time goes in v1:
time: 288 us; the launch traced here: 282 us
  matrix products  89.1 us (31%)
  blocking collectives  83.7 us (29%)
  local copies, waits for them, and re-layouts  55.7 us (19%)
  other arithmetic  18 us (6%)
  waiting for transfers between devices  16.6 us (6%)
  starting transfers between devices  16.1 us (6%)
    dot_general x40, matrix products, one_one_block(): jnp.dot(block_query, single_key.T, preferred_element_type=jnp.float32)  41.5 us
    dot_general x40, matrix products, one_one_block(): jnp.dot(shares, single_value, preferred_element_type=jnp.float32)  37.9 us
    unnamed x43, local copies, waits for them, and re-layouts  33.2 us
    all_to_all x1, blocking collectives, on_device(): lax.all_to_all(jnp.stack(jnp.split(result, lax.axis_size('rows'), axis=0)...  24 us
    psum x1, blocking collectives, on_device(): lax.psum((table_hot[:, None] * first_local[None, :], table_hot * count_lo...  23.4 us
    psum x1, blocking collectives, on_device(): second_sum = lax.psum(table_hot[:, None] * second_local[None, :], 'rows')  17.1 us
    all_to_all x1, waiting for transfers between devices, on_device(): lax.all_to_all(normed, 'feat', split_axis=0, concat_axis=1, tiled=True)  11 us
    all_gather x1, blocking collectives, on_device(): every_value = lax.all_gather(local_value, 'feat', axis=0, tiled=True)  10.2 us
  transfers between devices with their start and end apart: 4, of which 2 were waited for; matrix products, arithmetic and copies ran while one was open for 8% of the time, Pallas kernels for 0%

profile of v1, /device:TPU:0, one launch (start us, length us, event | category | flops | bytes accessed | tf_op | source)
XLA Modules:
  0.0 282.1 jit_solution(13969307917819574657)
XLA Ops:
  7.2 23.4 %all-reduce = (f32[8,20]{1,0:T(8,128)S(1)}, f32[8]{0:T(128)S(1)}) all-reduce(f32[8,20]{1,0:T(8,128)S(1)} %broadcast_multiply_fusion.1, f32[8]{0:T(128)S(1)} %compare_select_fusion.2), channel_id=1, replica_groups=mesh['rows'=8,'feat'=4] {'rows'}, use_global_device_ids=true, to_apply=%region_1.2 | all-reduce | flops 168 | bytes 1344 | tf_op jit(solution)/shard_map/psum | solution.py:75
  31.3 1.7 fusion.38
  33.0 17.1 %psum.23 = f32[8,20]{1,0:T(8,128)S(1)} all-reduce(f32[8,20]{1,0:T(8,128)S(1)} %broadcast_multiply_fusion), channel_id=1, replica_groups=mesh['rows'=8,'feat'=4] {'rows'}, use_global_device_ids=true, to_apply=%region_5.6 | all-reduce | flops 160 | bytes 1280 | tf_op jit(solution)/shard_map/psum | solution.py:82
  50.2 2.5 fusion.39
  52.7 3.5 %all-to-all-start = ((bf16[128,20,128]{2,1,0:T(8,128)(2,1)}), bf16[128,20,128]{2,1,0:T(8,128)(2,1)S(1)}, u32[]{:S(2)}, u32[]{:S(2)}) async-start(bf16[128,20,128]{2,1,0:T(8,128)(2,1)} %fusion.39), calls=%async_computation | async-start | bytes 1572864 | tf_op jit(solution)/shard_map/all_to_all | solution.py:86
  56.8 11.0 %all-to-all-done = bf16[128,20,128]{2,1,0:T(8,128)(2,1)S(1)} async-done(((bf16[128,20,128]{2,1,0:T(8,128)(2,1)}), bf16[128,20,128]{2,1,0:T(8,128)(2,1)S(1)}, u32[]{:S(2)}, u32[]{:S(2)}) %all-to-all-start) | async-done | bytes 655392 | tf_op jit(solution)/shard_map/all_to_all | solution.py:86
  71.5 10.6 %while.25 = (s32[]{:T(128)}, bf16[2,16,80,4,32]{2,4,3,1,0:T(8,128)(2,1)}, bf16[2,16,80,4,32]{2,4,3,1,0:T(8,128)(2,1)}, bf16[2,16,80,4,32]{2,4,3,1,0:T(8,128)(2,1...) while((s32[]{:T(128)}, bf16[2,16,80,4,32]{2,4,3,1,0:T(8,128)(2,1)}, ...), condition=%wide.region_9.10_spmd, body=%wide.region_6.9_spmd.sunk | while | flops 55050320 | bytes 12310625 | solution.py:49
  72.1 3.4 %fusion.87 = (f32[16,4,80]{2,1,0:T(4,128)S(1)}, f32[16,4,80,80]{2,3,1,0:T(8,128)S(1)}) fusion(f32[16,4,80,80]{2,3,1,0:T(8,128)S(1)} %fusion.86), kind=kOutput, calls=%fused_computation.105.clone.1 | output fusion | flops 1638479 | bytes 3297280 | tf_op jit(solution)/shard_map/while/body/eval_jaxpr/sub | solution.py:41
  77.4 3.4 %fusion.87 = (f32[16,4,80]{2,1,0:T(4,128)S(1)}, f32[16,4,80,80]{2,3,1,0:T(8,128)S(1)}) fusion(f32[16,4,80,80]{2,3,1,0:T(8,128)S(1)} %fusion.86), kind=kOutput, calls=%fused_computation.105.clone.1 | output fusion | flops 1638479 | bytes 3297280 | tf_op jit(solution)/shard_map/while/body/eval_jaxpr/sub | solution.py:41
  82.1 1.7 fusion.41
  86.1 3.4 %all-to-all-start.2 = ((bf16[8,2,2560]{2,1,0:T(2,128)(2,1)}), bf16[8,2,2560]{2,1,0:T(2,128)(2,1)S(1)}, u32[]{:S(2)}, u32[]{:S(2)}) async-start(bf16[8,2,2560]{2,1,0:T(2,128)(2,1)} %reshape.229), calls=%async_computation.2 | async-start | bytes 163840 | tf_op jit(solution)/shard_map/all_to_all | solution.py:126
  90.8 5.6 %all-to-all-done.2 = bf16[8,2,2560]{2,1,0:T(2,128)(2,1)S(1)} async-done(((bf16[8,2,2560]{2,1,0:T(2,128)(2,1)}), bf16[8,2,2560]{2,1,0:T(2,128)(2,1)S(1)}, u32[]{:S(2)}, u32[]{:S(2)}) %all-to-all-start.2) | async-done | bytes 81952 | tf_op jit(solution)/shard_map/all_to_all | solution.py:126
  96.4 3.4 %all-to-all-start.3 = ((bf16[8,2,2560]{2,1,0:T(2,128)(2,1)}), bf16[8,2,2560]{2,1,0:T(2,128)(2,1)S(1)}, u32[]{:S(2)}, u32[]{:S(2)}) async-start(bf16[8,2,2560]{2,1,0:T(2,128)(2,1)} %reshape.231), calls=%async_computation.3 | async-start | bytes 163840 | tf_op jit(solution)/shard_map/all_to_all | solution.py:127
  100.9 3.1 %reshape.208 = bf16[32,8,40,32]{3,2,1,0:T(8,128)(2,1)S(1)} reshape(bf16[32,80,128]{2,1,0:T(8,128)(2,1)} %convolution_convert_fusion.2) | data formatting | bytes 1310720 | tf_op jit(solution)/shard_map/reshape | solution.py:103
  104.0 2.5 copy.109
  106.5 5.8 %reshape.227 = bf16[8,2,20480]{2,1,0:T(2,128)(2,1)} reshape(bf16[8,32,32,40]{3,2,1,0:T(8,128)(2,1)} %bitcast.184) | data formatting | bytes 1310720
  112.9 5.9 %all-to-all-start.1 = ((bf16[8,2,20480]{2,1,0:T(2,128)(2,1)}), bf16[8,2,20480]{2,1,0:T(2,128)(2,1)S(1)}, u32[]{:S(2)}, u32[]{:S(2)}) async-start(bf16[8,2,20480]{2,1,0:T(2,128)(2,1)} %reshape.227), calls=%async_computation.1 | async-start | bytes 1310720 | tf_op jit(solution)/shard_map/all_to_all | solution.py:125
  120.1 9.1 %all_gather.6 = bf16[128,1,40,32]{2,3,1,0:T(8,128)(2,1)S(1)} all-gather(bf16[32,1,40,32]{2,3,1,0:T(8,128)(2,1)S(1)} %bitcast.192), channel_id=1, replica_groups=mesh['rows'=8,'feat'=4] {'feat'}, dimensions={0}, use_global_device_ids=true | all-gather | bytes 409600 | tf_op jit(solution)/shard_map/all_gather | solution.py:128
  129.2 2.9 %copy.116 = bf16[40,128,32]{2,1,0:T(8,128)(2,1)} copy(bf16[40,128,32]{0,2,1:T(8,128)(2,1)S(1)} %bitcast.188) | data formatting | bytes 655360
  132.5 10.2 %all_gather.7 = bf16[128,1,40,32]{2,3,1,0:T(8,128)(2,1)S(1)} all-gather(bf16[32,1,40,32]{2,3,1,0:T(8,128)(2,1)S(1)} %bitcast.193), channel_id=1, replica_groups=mesh['rows'=8,'feat'=4] {'feat'}, dimensions={0}, use_global_device_ids=true | all-gather | bytes 409600 | tf_op jit(solution)/shard_map/all_gather | solution.py:129
  142.7 2.9 %copy.117 = bf16[40,128,32]{2,1,0:T(8,128)(2,1)} copy(bf16[40,128,32]{0,2,1:T(8,128)(2,1)S(1)} %bitcast.189) | data formatting | bytes 655360
  145.5 3.3 %reshape.228 = bf16[8,32,32,40]{3,2,1,0:T(8,128)(2,1)S(1)} reshape(bf16[8,2,20480]{2,1,0:T(2,128)(2,1)S(1)} %all-to-all-done.1) | data formatting | bytes 1310720
  148.9 4.9 %copy.115 = bf16[40,256,32]{2,1,0:T(8,128)(2,1)} copy(bf16[40,256,32]{0,2,1:T(8,128)(2,1)S(1)} %bitcast.185) | data formatting | bytes 1310720
  153.8 81.5 %while.26 = (s32[]{:T(128)}, bf16[40,256,32]{1,2,0:T(8,128)(2,1)S(1)}, bf16[40,256,32]{2,1,0:T(8,128)(2,1)}, bf16[40,128,32]{2,1,0:T(8,128)(2,1)}, bf16[40,128,3...) while((s32[]{:T(128)}, ...), condition=%wide.region_16.17_spmd.clone, body=%wide.region_13.16_spmd.clone.sunk | while | flops 4529666 | bytes 549597 | solution.py:155
  235.3 3.5 %copy.118 = bf16[40,256,32]{0,2,1:T(8,128)(2,1)S(1)} copy(bf16[40,256,32]{1,2,0:T(8,128)(2,1)S(1)} %get-tuple-element.83) | data formatting | bytes 1310720 | tf_op jit(solution)/shard_map/while | solution.py:155
  240.5 5.0 %reshape.233 = bf16[8,2,20480]{2,1,0:T(2,128)(2,1)S(1)} reshape(bf16[8,32,1,32,40]{4,3,2,1,0:T(8,128)(2,1)} %bitcast.191) | data formatting | bytes 1310720
  245.5 24.0 %all_to_all.74 = bf16[8,2,20480]{2,1,0:T(2,128)(2,1)S(1)} all-to-all(bf16[8,2,20480]{2,1,0:T(2,128)(2,1)S(1)} %reshape.233), channel_id=1, replica_groups=mesh['rows'=8,'feat'=4] {'rows'}, dimensions={0} | all-to-all | bytes 1310720 | tf_op jit(solution)/shard_map/all_to_all | solution.py:157
  269.5 3.3 %reshape.234 = bf16[8,32,1,32,40]{4,3,2,1,0:T(8,128)(2,1)S(1)} reshape(bf16[8,2,20480]{2,1,0:T(2,128)(2,1)S(1)} %all_to_all.74) | data formatting | bytes 1310720
  272.8 1.8 bitcast_bitcast_fusion
  274.6 3.2 %copy.126 = bf16[32,8,1,40,32]{4,3,1,0,2:T(8,128)(2,1)S(1)} copy(bf16[32,8,1,40,32]{3,4,2,0,1:T(8,128)(2,1)} %bitcast_bitcast_fusion) | data formatting | bytes 1310720 | tf_op jit(solution)/shard_map/reshape | solution.py:156
  277.8 2.1 reshape_reshape.15
  279.9 2.2 fusion.42
  (211 shorter events, 103.7 us)
Async XLA Ops:
  0.0 67.9 %copy-start = (bf16[128,384]{1,0:T(8,128)(2,1)S(1)}, bf16[128,384]{1,0:T(8,128)(2,1)}, u32[]{:S(2)}) copy-start(bf16[128,384]{1,0:T(8,128)(2,1)} %param.16) | copy-start | bytes 294916
  5.5 50.6 %copy-start.11 = (s32[1024]{0:T(1024)S(1)}, s32[1024]{0:T(1024)}, u32[]{:S(2)}) copy-start(s32[1024]{0:T(1024)} %param.15) | copy-start | bytes 12292
  52.7 15.1 %all-to-all-start = ((bf16[128,20,128]{2,1,0:T(8,128)(2,1)}), bf16[128,20,128]{2,1,0:T(8,128)(2,1)S(1)}, u32[]{:S(2)}, u32[]{:S(2)}) async-start(bf16[128,20,128]{2,1,0:T(8,128)(2,1)} %fusion.39), calls=%async_computation | async-start | bytes 1572864 | tf_op jit(solution)/shard_map/all_to_all | solution.py:86
  71.5 10.6 %copy-start.9 = (bf16[128,128]{1,0:T(8,128)(2,1)S(1)}, bf16[128,128]{1,0:T(8,128)(2,1)}, u32[]{:S(2)}) copy-start(bf16[128,128]{1,0:T(8,128)(2,1)} %param.17) | copy-start | bytes 98308
  72.1 3.4 %copy-start.2 = (bf16[2,16,80,4,32]{2,4,3,1,0:T(8,128)(2,1)S(1)}, bf16[2,16,80,4,32]{2,4,3,1,0:T(8,128)(2,1)}, u32[]{:S(2)}) copy-start(bf16[2,16,80,4,32]{2,4,3,1,0:T(8,128)(2,1)} %get-tuple-element.283) | copy-start | bytes 1966084 | tf_op jit(solution)/shard_map/while
  77.4 3.4 %copy-start.2 = (bf16[2,16,80,4,32]{2,4,3,1,0:T(8,128)(2,1)S(1)}, bf16[2,16,80,4,32]{2,4,3,1,0:T(8,128)(2,1)}, u32[]{:S(2)}) copy-start(bf16[2,16,80,4,32]{2,4,3,1,0:T(8,128)(2,1)} %get-tuple-element.283) | copy-start | bytes 1966084 | tf_op jit(solution)/shard_map/while
  82.1 2.3 copy-start.8
  86.1 10.3 %all-to-all-start.2 = ((bf16[8,2,2560]{2,1,0:T(2,128)(2,1)}), bf16[8,2,2560]{2,1,0:T(2,128)(2,1)S(1)}, u32[]{:S(2)}, u32[]{:S(2)}) async-start(bf16[8,2,2560]{2,1,0:T(2,128)(2,1)} %reshape.229), calls=%async_computation.2 | async-start | bytes 163840 | tf_op jit(solution)/shard_map/all_to_all | solution.py:126
  96.4 3.4 %copy-start.4 = (bf16[8,2,2560]{2,1,0:T(2,128)(2,1)}, bf16[8,2,2560]{2,1,0:T(2,128)(2,1)S(1)}, u32[]{:S(2)}) copy-start(bf16[8,2,2560]{2,1,0:T(2,128)(2,1)S(1)} %all-to-all-done.2) | copy-start | bytes 245764
  96.4 15.8 %all-to-all-start.3 = ((bf16[8,2,2560]{2,1,0:T(2,128)(2,1)}), bf16[8,2,2560]{2,1,0:T(2,128)(2,1)S(1)}, u32[]{:S(2)}, u32[]{:S(2)}) async-start(bf16[8,2,2560]{2,1,0:T(2,128)(2,1)} %reshape.231), calls=%async_computation.3 | async-start | bytes 163840 | tf_op jit(solution)/shard_map/all_to_all | solution.py:127
  106.5 12.9 %copy-start.12 = (s32[8]{0:T(128)S(1)}, s32[8]{0:T(128)}, u32[]{:S(2)}) copy-start(s32[8]{0:T(128)} %param.13) | copy-start | bytes 100
  106.5 13.2 %copy-start.5 = (bf16[8,2,2560]{2,1,0:T(2,128)(2,1)S(1)}, bf16[8,2,2560]{2,1,0:T(2,128)(2,1)}, u32[]{:S(2)}) copy-start(bf16[8,2,2560]{2,1,0:T(2,128)(2,1)} %copy-done.4) | copy-start | bytes 245764
  112.2 0.6 copy-start.6
  112.9 32.7 %all-to-all-start.1 = ((bf16[8,2,20480]{2,1,0:T(2,128)(2,1)}), bf16[8,2,20480]{2,1,0:T(2,128)(2,1)S(1)}, u32[]{:S(2)}, u32[]{:S(2)}) async-start(bf16[8,2,20480]{2,1,0:T(2,128)(2,1)} %reshape.227), calls=%async_computation.1 | async-start | bytes 1310720 | tf_op jit(solution)/shard_map/all_to_all | solution.py:125
  118.8 13.3 %copy-start.7 = (bf16[8,2,2560]{2,1,0:T(2,128)(2,1)S(1)}, bf16[8,2,2560]{2,1,0:T(2,128)(2,1)}, u32[]{:S(2)}) copy-start(bf16[8,2,2560]{2,1,0:T(2,128)(2,1)} %copy-done.6) | copy-start | bytes 245764
  148.9 4.9 %copy-start.3 = (bf16[40,256,32]{1,2,0:T(8,128)(2,1)S(1)}, bf16[40,256,32]{1,2,0:T(8,128)(2,1)}, u32[]{:S(2)}) copy-start(bf16[40,256,32]{1,2,0:T(8,128)(2,1)} %custom-call.4) | copy-start | bytes 1966084
  239.1 1.4 copy-start.1
  277.8 2.1 copy-start.10
